TPU v7x, 32 devices: a whole 2x2x4 slice. The times are simulated.
32 devices in a mesh: row: 4 (over y, x), col: 8 (over z, core).
Axes of the slice: x: 2, y: 2, z: 4, core: 2. Of those that a mesh axis runs over, the one named last changes fastest.
Arguments:
- left_tiles: bfloat16 [2, 32, 256, 256], P(None, 'row', 'col'), may hold values from 0.02 to 3, as said below
- right_tile_store: bfloat16 [32, 24, 256, 256], P('col', 'row'), may hold values from 0.019897461 to 1
- right_index: int32 [32, 24], P('col', 'row'), may hold values from 0 to 7, as said below
- right_count: int32 [32, 4], P('col', 'row'), may hold values from 1 to 6
Outputs:
- inflated: bfloat16 [2, 32, 256, 256], P(None, 'col', 'row')
Inputs may be any that keep to these rules, and one draw needn't show every extreme that they name: `right_index`: for each column block and each row index the 6 slots name distinct contraction blocks; only the first right_count of them are used. `left_tiles`: positive entries.
All inputs are finite; a program needn't handle non-finite values.
Results may differ from a plain program's by a relative error of at most 0.001.
Values may be sent and summed in bfloat16 or wider, within the bound.
No kernel may reach another device: no remote copies, remote signals or barrier semaphores. Data moves between devices by JAX's collectives and lax.ppermute only.
A program may use at most 64 MiB of HBM per device.

v0:
```python
import jax
import jax.numpy as jnp
from jax import lax
from jax.sharding import PartitionSpec as P


def shards(left_tiles, right_tile_store, right_index, right_count):
    column_blocks = right_tile_store.shape[0]
    slot_total = right_tile_store.shape[1]
    window_blocks = left_tiles.shape[0]
    tile_size = right_tile_store.shape[2]
    live_mask = (jnp.arange(slot_total, dtype=jnp.int32)[None, :] < right_count).astype(
        jnp.bfloat16
    )
    flat_index = right_index.reshape(-1)
    shard_rows = lax.all_gather(left_tiles, "col", axis=2, tiled=True)
    picked = jnp.take(shard_rows, flat_index, axis=1)
    picked = picked.reshape(
        window_blocks, column_blocks, slot_total, shard_rows.shape[2], shard_rows.shape[3]
    )
    picked = picked * live_mask[None, :, :, None, None]
    partial_value = jnp.einsum(
        "ajqmb,jqbn->ajmn", picked, right_tile_store, preferred_element_type=jnp.float32
    )
    share = lax.psum_scatter(partial_value, "row", scatter_dimension=2, tiled=True)
    squared = share * share
    column_sums = lax.psum(jnp.sum(squared, axis=(0, 2)), "row")
    scaled = squared * (window_blocks * tile_size / column_sums[None, :, None, :])
    return scaled.astype(jnp.bfloat16)


def solution(mesh):
    in_specs = (
        P(None, "row", "col", None),
        P("col", "row", None, None),
        P("col", "row"),
        P("col", "row"),
    )
    out_specs = P(None, "col", "row", None)
    return jax.shard_map(shards, mesh=mesh, in_specs=in_specs, out_specs=out_specs, check_vma=False)
```

profile of v0, /device:TPU:0, one launch (start us, length us, event | category | flops | bytes accessed | tf_op | source)
XLA Modules:
  0.0 106.3 jit_solution(15490569830004205076)
XLA Ops:
  6.5 0.0 copy-start
  6.5 0.0 all-gather.2.cloned.1.call-start
  6.5 0.7 all-gather.2.cloned.1.call-update
  7.3 0.0 reduce-scatter.2.cloned.1.call-start
  7.3 0.9 reshape.66
  8.3 0.8 fusion.12
  9.0 31.8 %all-gather.2.cloned.1.call-done = bf16[2,8,256,256]{3,2,1,0:T(8,128)(2,1)} async-done(((bf16[2,8,32,256]{3,2,1,0:T(8,128)(2,1)}), bf16[2,8,256,256]{3,2,1,0:T(8,128)(2,1)}) %all-gather.2.cloned.1.call-update) | async-done | bytes 2097168 | tf_op jit(solution)/shard_map/all_gather | solution.py:16
  40.8 6.0 %gather_fusion = bf16[24,2,256,256]{3,2,1,0:T(8,128)(2,1)} fusion(bf16[2,8,256,256]{3,2,1,0:T(8,128)(2,1)} %all-gather.2.cloned.1.call-done, s32[1024]{0:T(1024)S(1)} %pad_clamp_fusion), kind=kCustom, calls=%fused_computation | custom fusion | bytes 12583008 | tf_op jit(solution)/shard_map/jit(_take)/gather | solution.py:17
  46.8 0.0 copy-done
  46.8 6.0 %fusion.7 = f32[2,4,256,256]{3,2,0,1:T(8,128)} fusion(bf16[4,6,256,256]{3,2,1,0:T(8,128)(2,1)S(1)} %copy-done, bf16[2,4,6,256,256]{4,3,0,2,1:T(8,128)(2,1)} %bitcast.18, pred[4,6]{1,0:T(4,128)(4,1)S(1)} %get-tuple-element.6, bf16[4,6]{1,0:T(4,128)(2,1)S(1)} %get-tuple-element.5), kind=kOutput, calls=%fused_computation.8 | convolution fusion | flops 1616904192 | bytes 11534408 | tf_op jit(solution)/shard_map/ajqmb,jqbn->ajmn/dot_general | solution.py:22
  52.8 0.0 reduce-scatter.2.cloned.1.call-update
  52.8 34.7 %reduce-scatter.2.cloned.1.call-done = f32[2,4,64,256]{3,2,0,1:T(8,128)} async-done(((f32[2,4,256,256]{3,2,0,1:T(8,128)}), f32[2,4,64,256]{3,2,0,1:T(8,128)}) %reduce-scatter.2.cloned.1.call-update) | async-done | bytes 524304 | tf_op jit(solution)/shard_map/reduce_scatter | solution.py:25
  87.6 1.1 %multiply_reduce_fusion = f32[4,256]{1,0:T(4,128)S(1)} fusion(f32[2,4,64,256]{3,2,0,1:T(8,128)} %reduce-scatter.2.cloned.1.call-done), kind=kLoop, calls=%fused_computation.10 | loop fusion | flops 261120 | bytes 528384 | tf_op jit(solution)/shard_map/reduce_sum | solution.py:27
  88.7 9.0 %psum.7 = f32[4,256]{1,0:T(4,128)S(1)} all-reduce(f32[4,256]{1,0:T(4,128)S(1)} %multiply_reduce_fusion), channel_id=1, replica_groups=mesh['row'=4,'col'=8] {'row'}, use_global_device_ids=true, to_apply=%region_2.3 | all-reduce | flops 1024 | bytes 8192 | tf_op jit(solution)/shard_map/psum | solution.py:27
  97.6 1.1 %multiply_convert_fusion = bf16[2,4,64,256]{3,2,0,1:T(8,128)(2,1)S(1)} fusion(f32[2,4,64,256]{3,2,0,1:T(8,128)} %reduce-scatter.2.cloned.1.call-done, f32[4,256]{1,0:T(4,128)S(1)} %broadcast_divide_fusion), kind=kLoop, calls=%fused_computation.9 | loop fusion | flops 393216 | bytes 790528 | tf_op jit(solution)/shard_map/convert_element_type | solution.py:29
  98.7 0.7 copy.6
  (3 shorter events, 0.0 us)
Async XLA Ops:
  6.5 40.3 %copy-start = (bf16[4,6,256,256]{3,2,1,0:T(8,128)(2,1)S(1)}, bf16[4,6,256,256]{3,2,1,0:T(8,128)(2,1)}, u32[]{:S(2)}) copy-start(bf16[4,6,256,256]{3,2,1,0:T(8,128)(2,1)} %param.5) | copy-start | bytes 9437188
  6.5 34.3 %all-gather.2.cloned.1.call-start = ((), (), s32[]{:S(2)}) async-start(), calls=%async_computation.1 | async-start | bytes 2359296 | tf_op jit(solution)/shard_map/all_gather | solution.py:16
  7.3 80.3 %reduce-scatter.2.cloned.1.call-start = ((), (), s32[]{:S(2)}) async-start(), calls=%async_computation.2 | async-start | bytes 2621440 | tf_op jit(solution)/shard_map/reduce_scatter | solution.py:25
Sparse Core Ops, SparseCore 0:
  8.9 31.8 all-gather.1
  52.9 34.5 reduce-scatter.1
where the time goes:
time: 107 us; the launch traced here: 106 us
  waiting for transfers between devices  67.3 us (63%)
  between operations  13.4 us (13%)
  blocking collectives  8.97 us (8%)
  local copies, waits for them, and re-layouts  7.65 us (7%)
  matrix products  5.96 us (6%)
  other arithmetic  2.98 us (3%)
    reduce_scatter x1, waiting for transfers between devices, shards(): lax.psum_scatter(partial_value, 'row', scatter_dimension=2, tiled=True)  34.7 us
    all_gather x1, waiting for transfers between devices, shards(): shard_rows = lax.all_gather(left_tiles, 'col', axis=2, tiled=True)  31.8 us
    psum x1, blocking collectives, shards(): column_sums = lax.psum(jnp.sum(squared, axis=(0, 2)), 'row')  8.97 us
    gather x1, local copies, waits for them, and re-layouts, shards(): picked = jnp.take(shard_rows, flat_index, axis=1)  5.99 us
    dot_general x1, matrix products, shards(): jnp.einsum('ajqmb,jqbn->ajmn', picked, right_tile_store, preferred_elemen...  5.96 us
  transfers between devices with their start and end apart: 2, of which 2 were waited for; matrix products, arithmetic and copies ran while one was open for 2% of the time, Pallas kernels for 0%

commit v1 on v0

--- a/solution.py
+++ b/solution.py
@@ -13,7 +13,12 @@
         jnp.bfloat16
     )
     flat_index = right_index.reshape(-1)
-    shard_rows = lax.all_gather(left_tiles, "col", axis=2, tiled=True)
+    ring = [left_tiles]
+    for hop in range(7):
+        ring.append(lax.ppermute(ring[-1], "col", [(dev, (dev + 1) % 8) for dev in range(8)]))
+    shard_rows = jnp.roll(
+        jnp.concatenate(ring[::-1], axis=2), (lax.axis_index("col") + 1) * ring[0].shape[2], axis=2
+    )
     picked = jnp.take(shard_rows, flat_index, axis=1)
     picked = picked.reshape(
         window_blocks, column_blocks, slot_total, shard_rows.shape[2], shard_rows.shape[3]

time: 107 us -> 142 us (1.33)
  waiting for transfers between devices: 67.3 us -> 87 us
  local copies, waits for them, and re-layouts: 7.65 us -> 22.6 us
    ppermute x0 -> x7, waiting for transfers between devices: none -> 52.9 us  [shards(): lax.ppermute(ring[-1], 'col', [(dev, (dev + 1) % 8) for dev in range(8)])]
    all_gather x1 -> x0, waiting for transfers between devices: 31.8 us -> none  [shards(): shard_rows = lax.all_gather(left_tiles, 'col', axis=2, tiled=True)]
    unnamed x2 -> x35, local copies, waits for them, and re-layouts: 0.01 us -> 13.6 us
    dynamic_slice x0 -> x1, local copies, waits for them, and re-layouts: none -> 1.49 us  [shards(): jnp.roll(jnp.concatenate(ring[::-1], axis=2), (lax.axis_index('col') + 1)...]
  transfers between devices with their start and end apart: 2 -> 8, of which waited for: 2 -> 8; matrix products, arithmetic and copies ran while one was open for 2% -> 1% of each run, Pallas kernels for 0% -> 0%
where the time goes in v1:
time: 142 us
  waiting for transfers between devices  87 us (61%)
  local copies, waits for them, and re-layouts  22.6 us (16%)
  between operations  13.6 us (10%)
  blocking collectives  8.94 us (6%)
  matrix products  5.95 us (4%)
  other arithmetic  3.06 us (2%)
    ppermute x7, waiting for transfers between devices, shards(): lax.ppermute(ring[-1], 'col', [(dev, (dev + 1) % 8) for dev in range(8)])  52.9 us
    reduce_scatter x1, waiting for transfers between devices, shards(): lax.psum_scatter(partial_value, 'row', scatter_dimension=2, tiled=True)  34 us
    unnamed x35, local copies, waits for them, and re-layouts  13.6 us
    psum x1, blocking collectives, shards(): column_sums = lax.psum(jnp.sum(squared, axis=(0, 2)), 'row')  8.94 us
    gather x1, local copies, waits for them, and re-layouts, shards(): picked = jnp.take(shard_rows, flat_index, axis=1)  5.98 us
    dot_general x1, matrix products, shards(): jnp.einsum('ajqmb,jqbn->ajmn', picked, right_tile_store, preferred_elemen...  5.95 us
  transfers between devices with their start and end apart: 8, of which 8 were waited for; matrix products, arithmetic and copies ran while one was open for 1% of the time, Pallas kernels for 0%

profile of v1, /device:TPU:0, one launch (start us, length us, event | category | flops | bytes accessed | tf_op | source)
XLA Modules:
  0.0 141.6 jit_solution(1844884422299429673)
XLA Ops:
  6.5 0.0 copy-start
  6.5 0.0 reduce-scatter.2.cloned.1.call-start
  6.5 0.5 collective-permute-start
  7.0 8.3 %collective-permute-done = bf16[2,8,32,256]{3,2,1,0:T(8,128)(2,1)S(1)} collective-permute-done((bf16[2,8,32,256]{3,2,1,0:T(8,128)(2,1)}, bf16[2,8,32,256]{3,2,1,0:T(8,128)(2,1)S(1)}, u32[]{:S(2)}, u32[]{:S(2)}) %collective-permute-start) | collective-permute-done | bytes 262176 | tf_op jit(solution)/shard_map/ppermute | solution.py:18
  15.4 0.7 copy-done.2
  16.1 0.0 collective-permute-start.1
  16.1 7.6 %collective-permute-done.1 = bf16[2,8,32,256]{3,2,1,0:T(8,128)(2,1)S(1)} collective-permute-done((bf16[2,8,32,256]{3,2,1,0:T(8,128)(2,1)S(1)}, bf16[2,8,32,256]{3,2,1,0:T(8,128)(2,1)S(1)}, u32[]{:S(2)}, u32[]{:S(2)}) %collective-permute-start.1) | collective-permute-done | bytes 262176 | tf_op jit(solution)/shard_map/ppermute | solution.py:18
  23.7 0.7 copy-done.4
  24.4 0.0 collective-permute-start.2
  24.4 7.6 %collective-permute-done.2 = bf16[2,8,32,256]{3,2,1,0:T(8,128)(2,1)S(1)} collective-permute-done((bf16[2,8,32,256]{3,2,1,0:T(8,128)(2,1)S(1)}, bf16[2,8,32,256]{3,2,1,0:T(8,128)(2,1)S(1)}, u32[]{:S(2)}, u32[]{:S(2)}) %collective-permute-start.2) | collective-permute-done | bytes 262176 | tf_op jit(solution)/shard_map/ppermute | solution.py:18
  32.0 0.7 copy-done.6
  32.7 0.0 collective-permute-start.3
  32.7 7.6 %collective-permute-done.3 = bf16[2,8,32,256]{3,2,1,0:T(8,128)(2,1)S(1)} collective-permute-done((bf16[2,8,32,256]{3,2,1,0:T(8,128)(2,1)S(1)}, bf16[2,8,32,256]{3,2,1,0:T(8,128)(2,1)S(1)}, u32[]{:S(2)}, u32[]{:S(2)}) %collective-permute-start.3) | collective-permute-done | bytes 262176 | tf_op jit(solution)/shard_map/ppermute | solution.py:18
  40.3 0.7 copy-done.8
  41.0 0.0 collective-permute-start.4
  41.0 7.7 %collective-permute-done.4 = bf16[2,8,32,256]{3,2,1,0:T(8,128)(2,1)} collective-permute-done((bf16[2,8,32,256]{3,2,1,0:T(8,128)(2,1)S(1)}, bf16[2,8,32,256]{3,2,1,0:T(8,128)(2,1)}, u32[]{:S(2)}, u32[]{:S(2)}) %collective-permute-start.4) | collective-permute-done | bytes 262176 | tf_op jit(solution)/shard_map/ppermute | solution.py:18
  48.7 0.0 collective-permute-start.5
  48.7 0.8 reshape.66
  49.4 7.1 %collective-permute-done.5 = bf16[2,8,32,256]{3,2,1,0:T(8,128)(2,1)} collective-permute-done((bf16[2,8,32,256]{3,2,1,0:T(8,128)(2,1)}, bf16[2,8,32,256]{3,2,1,0:T(8,128)(2,1)}, u32[]{:S(2)}, u32[]{:S(2)}) %collective-permute-start.5) | collective-permute-done | bytes 262176 | tf_op jit(solution)/shard_map/ppermute | solution.py:18
  56.6 0.0 collective-permute-start.6
  56.6 0.0 copy-start.9
  56.6 0.0 copy-start.7
  56.6 0.0 copy-start.5
  56.6 0.0 copy-start.3
  56.6 0.9 fusion.12
  57.5 7.0 %collective-permute-done.6 = bf16[2,8,32,256]{3,2,1,0:T(8,128)(2,1)} collective-permute-done((bf16[2,8,32,256]{3,2,1,0:T(8,128)(2,1)}, bf16[2,8,32,256]{3,2,1,0:T(8,128)(2,1)}, u32[]{:S(2)}, u32[]{:S(2)}) %collective-permute-start.6) | collective-permute-done | bytes 262176 | tf_op jit(solution)/shard_map/ppermute | solution.py:18
  64.5 1.0 constant_dynamic-update-slice_fusion.15
  65.5 1.0 constant_dynamic-update-slice_fusion.14
  66.4 1.0 constant_dynamic-update-slice_fusion.13
  67.4 1.0 constant_dynamic-update-slice_fusion.12
  68.4 1.0 constant_dynamic-update-slice_fusion.11
  69.3 1.0 constant_dynamic-update-slice_fusion.10
  70.3 1.0 constant_dynamic-update-slice_fusion.9
  71.3 1.0 constant_dynamic-update-slice_fusion.8
  72.3 1.0 constant_dynamic-update-slice_fusion.7
  73.2 1.0 constant_dynamic-update-slice_fusion.6
  74.2 1.0 constant_dynamic-update-slice_fusion.5
  75.2 0.0 copy-done.7
  75.3 0.0 copy-done.3
  75.4 1.5 %constant_dynamic-slice_fusion = bf16[2,8,256,256]{3,2,1,0:T(8,128)(2,1)} fusion(bf16[2,8,512,256]{3,2,1,0:T(8,128)(2,1)S(1)} %constant_dynamic-update-slice_fusion, s32[]{:T(128)S(6)} %select_n.37), kind=kLoop, calls=%fused_computation.35 | loop fusion | bytes 4194308 | tf_op jit(solution)/shard_map/jit(_roll_dynamic)/dynamic_slice | solution.py:19
  76.9 6.0 %gather_fusion = bf16[24,2,256,256]{3,2,1,0:T(8,128)(2,1)} fusion(bf16[2,8,256,256]{3,2,1,0:T(8,128)(2,1)} %constant_dynamic-slice_fusion, s32[1024]{0:T(1024)S(1)} %pad_clamp_fusion), kind=kCustom, calls=%fused_computation | custom fusion | bytes 12583008 | tf_op jit(solution)/shard_map/jit(_take)/gather | solution.py:22
  82.8 6.0 %fusion.7 = f32[2,4,256,256]{3,2,0,1:T(8,128)} fusion(bf16[4,6,256,256]{3,2,1,0:T(8,128)(2,1)S(1)} %copy-done, bf16[2,4,6,256,256]{4,3,0,2,1:T(8,128)(2,1)} %bitcast.18, pred[4,6]{1,0:T(4,128)(4,1)S(1)} %get-tuple-element.6, bf16[4,6]{1,0:T(4,128)(2,1)S(1)} %get-tuple-element.5), kind=kOutput, calls=%fused_computation.8 | convolution fusion | flops 1616904192 | bytes 11534408 | tf_op jit(solution)/shard_map/ajqmb,jqbn->ajmn/dot_general | solution.py:27
  88.8 0.0 reduce-scatter.2.cloned.1.call-update
  88.8 34.0 %reduce-scatter.2.cloned.1.call-done = f32[2,4,64,256]{3,2,0,1:T(8,128)} async-done(((f32[2,4,256,256]{3,2,0,1:T(8,128)}), f32[2,4,64,256]{3,2,0,1:T(8,128)}) %reduce-scatter.2.cloned.1.call-update) | async-done | bytes 524304 | tf_op jit(solution)/shard_map/reduce_scatter | solution.py:30
  122.9 1.1 multiply_reduce_fusion
  124.0 8.9 %psum.7 = f32[4,256]{1,0:T(4,128)S(1)} all-reduce(f32[4,256]{1,0:T(4,128)S(1)} %multiply_reduce_fusion), channel_id=1, replica_groups=mesh['row'=4,'col'=8] {'row'}, use_global_device_ids=true, to_apply=%region_2.3 | all-reduce | flops 1024 | bytes 8192 | tf_op jit(solution)/shard_map/psum | solution.py:32
  132.9 1.1 multiply_convert_fusion
  134.0 0.7 copy.6
  (17 shorter events, 0.1 us)
Async XLA Ops:
  6.5 76.3 %copy-start = (bf16[4,6,256,256]{3,2,1,0:T(8,128)(2,1)S(1)}, bf16[4,6,256,256]{3,2,1,0:T(8,128)(2,1)}, u32[]{:S(2)}) copy-start(bf16[4,6,256,256]{3,2,1,0:T(8,128)(2,1)} %param.5) | copy-start | bytes 9437188
  6.5 68.8 %copy-start.1 = (bf16[2,8,32,256]{3,2,1,0:T(8,128)(2,1)S(1)}, bf16[2,8,32,256]{3,2,1,0:T(8,128)(2,1)}, u32[]{:S(2)}) copy-start(bf16[2,8,32,256]{3,2,1,0:T(8,128)(2,1)} %param.4) | copy-start | bytes 786436
  6.5 116.3 %reduce-scatter.2.cloned.1.call-start = ((), (), s32[]{:S(2)}) async-start(), calls=%async_computation.1 | async-start | bytes 2621440 | tf_op jit(solution)/shard_map/reduce_scatter | solution.py:30
  6.5 8.8 %collective-permute-start = (bf16[2,8,32,256]{3,2,1,0:T(8,128)(2,1)}, bf16[2,8,32,256]{3,2,1,0:T(8,128)(2,1)S(1)}, u32[]{:S(2)}, u32[]{:S(2)}) collective-permute-start(bf16[2,8,32,256]{3,2,1,0:T(8,128)(2,1)} %param.4), channel_id=1, source_target_pairs={{0,1},{1,2},{2,3},{3,4},{4,5},{5,6},{6,7},{7,0},{8,9},{9,10},{10,1... | collective-permute-start | bytes 786440 | tf_op jit(solution)/shard_map/ppermute | solution.py:18
  15.4 0.7 copy-start.2
  16.1 7.6 %collective-permute-start.1 = (bf16[2,8,32,256]{3,2,1,0:T(8,128)(2,1)S(1)}, bf16[2,8,32,256]{3,2,1,0:T(8,128)(2,1)S(1)}, u32[]{:S(2)}, u32[]{:S(2)}) collective-permute-start(bf16[2,8,32,256]{3,2,1,0:T(8,128)(2,1)S(1)} %collective-permute-done), channel_id=1, source_target_pairs={{0,1},{1,2},{2,3},{3,4},{4,5},{5,6},{6,7},{7,0},{8,9},{9,10},{10,1... | collective-permute-start | bytes 786440 | tf_op jit(solution)/shard_map/ppermute | solution.py:18
  23.7 0.7 copy-start.4
  24.4 7.6 %collective-permute-start.2 = (bf16[2,8,32,256]{3,2,1,0:T(8,128)(2,1)S(1)}, bf16[2,8,32,256]{3,2,1,0:T(8,128)(2,1)S(1)}, u32[]{:S(2)}, u32[]{:S(2)}) collective-permute-start(bf16[2,8,32,256]{3,2,1,0:T(8,128)(2,1)S(1)} %collective-permute-done.1), channel_id=1, source_target_pairs={{0,1},{1,2},{2,3},{3,4},{4,5},{5,6},{6,7},{7,0},{8,9},{9,10},{10,1... | collective-permute-start | bytes 786440 | tf_op jit(solution)/shard_map/ppermute | solution.py:18
  32.0 0.7 copy-start.6
  32.7 7.6 %collective-permute-start.3 = (bf16[2,8,32,256]{3,2,1,0:T(8,128)(2,1)S(1)}, bf16[2,8,32,256]{3,2,1,0:T(8,128)(2,1)S(1)}, u32[]{:S(2)}, u32[]{:S(2)}) collective-permute-start(bf16[2,8,32,256]{3,2,1,0:T(8,128)(2,1)S(1)} %collective-permute-done.2), channel_id=1, source_target_pairs={{0,1},{1,2},{2,3},{3,4},{4,5},{5,6},{6,7},{7,0},{8,9},{9,10},{10,1... | collective-permute-start | bytes 786440 | tf_op jit(solution)/shard_map/ppermute | solution.py:18
  40.3 0.7 copy-start.8
  41.0 7.7 %collective-permute-start.4 = (bf16[2,8,32,256]{3,2,1,0:T(8,128)(2,1)S(1)}, bf16[2,8,32,256]{3,2,1,0:T(8,128)(2,1)}, u32[]{:S(2)}, u32[]{:S(2)}) collective-permute-start(bf16[2,8,32,256]{3,2,1,0:T(8,128)(2,1)S(1)} %collective-permute-done.3), channel_id=1, source_target_pairs={{0,1},{1,2},{2,3},{3,4},{4,5},{5,6},{6,7},{7,0},{8,9},{9,10},{10,1... | collective-permute-start | bytes 786440 | tf_op jit(solution)/shard_map/ppermute | solution.py:18
  48.7 7.9 %collective-permute-start.5 = (bf16[2,8,32,256]{3,2,1,0:T(8,128)(2,1)}, bf16[2,8,32,256]{3,2,1,0:T(8,128)(2,1)}, u32[]{:S(2)}, u32[]{:S(2)}) collective-permute-start(bf16[2,8,32,256]{3,2,1,0:T(8,128)(2,1)} %collective-permute-done.4), channel_id=1, source_target_pairs={{0,1},{1,2},{2,3},{3,4},{4,5},{5,6},{6,7},{7,0},{8,9},{9,10},{10,1... | collective-permute-start | bytes 786440 | tf_op jit(solution)/shard_map/ppermute | solution.py:18
  56.6 7.9 %collective-permute-start.6 = (bf16[2,8,32,256]{3,2,1,0:T(8,128)(2,1)}, bf16[2,8,32,256]{3,2,1,0:T(8,128)(2,1)}, u32[]{:S(2)}, u32[]{:S(2)}) collective-permute-start(bf16[2,8,32,256]{3,2,1,0:T(8,128)(2,1)} %collective-permute-done.5), channel_id=1, source_target_pairs={{0,1},{1,2},{2,3},{3,4},{4,5},{5,6},{6,7},{7,0},{8,9},{9,10},{10,1... | collective-permute-start | bytes 786440 | tf_op jit(solution)/shard_map/ppermute | solution.py:18
  56.6 18.6 %copy-start.9 = (bf16[2,8,32,256]{3,2,1,0:T(8,128)(2,1)S(1)}, bf16[2,8,32,256]{3,2,1,0:T(8,128)(2,1)}, u32[]{:S(2)}) copy-start(bf16[2,8,32,256]{3,2,1,0:T(8,128)(2,1)} %copy-done.8) | copy-start | bytes 786436
  56.6 18.6 %copy-start.7 = (bf16[2,8,32,256]{3,2,1,0:T(8,128)(2,1)S(1)}, bf16[2,8,32,256]{3,2,1,0:T(8,128)(2,1)}, u32[]{:S(2)}) copy-start(bf16[2,8,32,256]{3,2,1,0:T(8,128)(2,1)} %copy-done.6) | copy-start | bytes 786436
  56.6 18.6 %copy-start.5 = (bf16[2,8,32,256]{3,2,1,0:T(8,128)(2,1)S(1)}, bf16[2,8,32,256]{3,2,1,0:T(8,128)(2,1)}, u32[]{:S(2)}) copy-start(bf16[2,8,32,256]{3,2,1,0:T(8,128)(2,1)} %copy-done.4) | copy-start | bytes 786436
  56.6 18.7 %copy-start.3 = (bf16[2,8,32,256]{3,2,1,0:T(8,128)(2,1)S(1)}, bf16[2,8,32,256]{3,2,1,0:T(8,128)(2,1)}, u32[]{:S(2)}) copy-start(bf16[2,8,32,256]{3,2,1,0:T(8,128)(2,1)} %copy-done.2) | copy-start | bytes 786436
Sparse Core Ops, SparseCore 0:
  88.9 33.8 reduce-scatter.1

commit v2 on v0

--- a/solution.py
+++ b/solution.py
@@ -24,7 +24,7 @@
     )
     share = lax.psum_scatter(partial_value, "row", scatter_dimension=2, tiled=True)
     squared = share * share
-    column_sums = lax.psum(jnp.sum(squared, axis=(0, 2)), "row")
+    column_sums = jnp.sum(lax.all_gather(jnp.sum(squared, axis=(0, 2)), "row"), axis=0)
     scaled = squared * (window_blocks * tile_size / column_sums[None, :, None, :])
     return scaled.astype(jnp.bfloat16)
 

time: 107 us -> 106 us (level)
    psum x1 -> x0, blocking collectives: 8.97 us -> none  [shards(): column_sums = lax.psum(jnp.sum(squared, axis=(0, 2)), 'row')]
    all_gather x0 -> x1, blocking collectives: none -> 8.16 us  [shards(): lax.all_gather(jnp.sum(squared, axis=(0, 2)), 'row')]
where the time goes in v2:
time: 106 us
  waiting for transfers between devices  67.3 us (63%)
  between operations  13.4 us (13%)
  blocking collectives  8.16 us (8%)
  local copies, waits for them, and re-layouts  7.65 us (7%)
  matrix products  5.96 us (6%)
  other arithmetic  2.99 us (3%)
    reduce_scatter x1, waiting for transfers between devices, shards(): lax.psum_scatter(partial_value, 'row', scatter_dimension=2, tiled=True)  34.7 us
    all_gather x1, waiting for transfers between devices, shards(): shard_rows = lax.all_gather(left_tiles, 'col', axis=2, tiled=True)  31.8 us
    all_gather x1, blocking collectives, shards(): lax.all_gather(jnp.sum(squared, axis=(0, 2)), 'row')  8.16 us
    gather x1, local copies, waits for them, and re-layouts, shards(): picked = jnp.take(shard_rows, flat_index, axis=1)  5.99 us
    dot_general x1, matrix products, shards(): jnp.einsum('ajqmb,jqbn->ajmn', picked, right_tile_store, preferred_elemen...  5.96 us
  transfers between devices with their start and end apart: 2, of which 2 were waited for; matrix products, arithmetic and copies ran while one was open for 2% of the time, Pallas kernels for 0%

profile of v2, /device:TPU:0, one launch (start us, length us, event | category | flops | bytes accessed | tf_op | source)
XLA Modules:
  0.0 105.5 jit_solution(14533464524063489275)
XLA Ops:
  6.5 0.0 copy-start
  6.5 0.0 all-gather.4.cloned.1.call-start
  6.5 0.7 all-gather.4.cloned.1.call-update
  7.3 0.0 reduce-scatter.2.cloned.1.call-start
  7.3 0.9 reshape.68
  8.3 0.8 fusion.12
  9.0 31.8 %all-gather.4.cloned.1.call-done = bf16[2,8,256,256]{3,2,1,0:T(8,128)(2,1)} async-done(((bf16[2,8,32,256]{3,2,1,0:T(8,128)(2,1)}), bf16[2,8,256,256]{3,2,1,0:T(8,128)(2,1)}) %all-gather.4.cloned.1.call-update) | async-done | bytes 2097168 | tf_op jit(solution)/shard_map/all_gather | solution.py:16
  40.8 6.0 %gather_fusion = bf16[24,2,256,256]{3,2,1,0:T(8,128)(2,1)} fusion(bf16[2,8,256,256]{3,2,1,0:T(8,128)(2,1)} %all-gather.4.cloned.1.call-done, s32[1024]{0:T(1024)S(1)} %pad_clamp_fusion), kind=kCustom, calls=%fused_computation | custom fusion | bytes 12583008 | tf_op jit(solution)/shard_map/jit(_take)/gather | solution.py:17
  46.8 0.0 copy-done
  46.8 6.0 %fusion.7 = f32[2,4,256,256]{3,2,0,1:T(8,128)} fusion(bf16[4,6,256,256]{3,2,1,0:T(8,128)(2,1)S(1)} %copy-done, bf16[2,4,6,256,256]{4,3,0,2,1:T(8,128)(2,1)} %bitcast.19, pred[4,6]{1,0:T(4,128)(4,1)S(1)} %get-tuple-element.6, bf16[4,6]{1,0:T(4,128)(2,1)S(1)} %get-tuple-element.5), kind=kOutput, calls=%fused_computation.8 | convolution fusion | flops 1616904192 | bytes 11534408 | tf_op jit(solution)/shard_map/ajqmb,jqbn->ajmn/dot_general | solution.py:22
  52.8 0.0 reduce-scatter.2.cloned.1.call-update
  52.8 34.7 %reduce-scatter.2.cloned.1.call-done = f32[2,4,64,256]{3,2,0,1:T(8,128)} async-done(((f32[2,4,256,256]{3,2,0,1:T(8,128)}), f32[2,4,64,256]{3,2,0,1:T(8,128)}) %reduce-scatter.2.cloned.1.call-update) | async-done | bytes 524304 | tf_op jit(solution)/shard_map/reduce_scatter | solution.py:25
  87.6 1.1 %multiply_reduce_fusion = f32[4,256]{1,0:T(4,128)S(1)} fusion(f32[2,4,64,256]{3,2,0,1:T(8,128)} %reduce-scatter.2.cloned.1.call-done), kind=kLoop, calls=%fused_computation.10 | loop fusion | flops 261120 | bytes 528384 | tf_op jit(solution)/shard_map/reduce_sum | solution.py:27
  88.7 8.2 %all-gather.1 = f32[4,4,256]{2,1,0:T(4,128)S(1)} all-gather(f32[1,4,256]{2,1,0:T(4,128)S(1)} %bitcast.20), channel_id=2, replica_groups=mesh['row'=4,'col'=8] {'row'}, dimensions={0}, use_global_device_ids=true | all-gather | bytes 20480 | tf_op jit(solution)/shard_map/all_gather | solution.py:27
  96.9 1.1 %multiply_convert_fusion = bf16[2,4,64,256]{3,2,0,1:T(8,128)(2,1)S(1)} fusion(f32[2,4,64,256]{3,2,0,1:T(8,128)} %reduce-scatter.2.cloned.1.call-done, f32[4,256]{1,0:T(4,128)S(1)} %broadcast_divide_fusion), kind=kLoop, calls=%fused_computation.9 | loop fusion | flops 393216 | bytes 790528 | tf_op jit(solution)/shard_map/convert_element_type | solution.py:29
  98.0 0.7 copy.8
  (4 shorter events, 0.0 us)
Async XLA Ops:
  6.5 40.3 %copy-start = (bf16[4,6,256,256]{3,2,1,0:T(8,128)(2,1)S(1)}, bf16[4,6,256,256]{3,2,1,0:T(8,128)(2,1)}, u32[]{:S(2)}) copy-start(bf16[4,6,256,256]{3,2,1,0:T(8,128)(2,1)} %param.5) | copy-start | bytes 9437188
  6.5 34.3 %all-gather.4.cloned.1.call-start = ((), (), s32[]{:S(2)}) async-start(), calls=%async_computation.1 | async-start | bytes 2359296 | tf_op jit(solution)/shard_map/all_gather | solution.py:16
  7.3 80.3 %reduce-scatter.2.cloned.1.call-start = ((), (), s32[]{:S(2)}) async-start(), calls=%async_computation.2 | async-start | bytes 2621440 | tf_op jit(solution)/shard_map/reduce_scatter | solution.py:25
Sparse Core Ops, SparseCore 0:
  8.9 31.8 all-gather.3
  52.9 34.5 reduce-scatter.1
